TPU v7x, 32 devices: a whole 2x2x4 slice. The times are simulated.
32 devices in a mesh: dp: 8 (over z, y), head: 4 (over x, core).
Axes of the slice: x: 2, y: 2, z: 4, core: 2. Of those that a mesh axis runs over, the one named last changes fastest.
Arguments:
- tokens: bfloat16 [8, 6312, 768], P('dp', 'head'), may hold values from -6 to 6
- frames: int32 [8], P('dp'), may hold values from 4 to 16
- text_mask: int32 [8, 40], P('dp'), may hold values 0 or 1
- latents: bfloat16 [8, 128, 768], P('dp'), may hold values from -6 to 6
- cross_q: bfloat16 [768, 768], P('head'), may hold values from -0.21875 to 0.21875
- cross_kv: bfloat16 [2, 768, 768], P(None, 'head'), may hold values from -0.21875 to 0.21875
- cross_out: bfloat16 [768, 768], P('head'), may hold values from -3.5 to 3.5
- cross_up: bfloat16 [768, 3072], P(None, 'head'), may hold values from -0.21875 to 0.21875
- cross_down: bfloat16 [3072, 768], P('head'), may hold values from -0.109375 to 0.109375
- self_qkv: bfloat16 [3, 768, 768], P(None, 'head'), may hold values from -0.21875 to 0.21875
- self_out: bfloat16 [768, 768], P('head'), may hold values from -0.875 to 0.875
- self_up: bfloat16 [768, 3072], P(None, 'head'), may hold values from -0.21875 to 0.21875
- self_down: bfloat16 [3072, 768], P('head'), may hold values from -0.109375 to 0.109375
- head_bias: float32 [2, 2, 768], P(None, None, 'head'), may hold values from -1.8 to 1.8
- up_bias: float32 [2, 3072], P(None, 'head'), may hold values from -1.8 to 1.8
- out_bias: float32 [2, 2, 768], replicated, may hold values from -1.8 to 1.8
- norm_gain: float32 [5, 768], replicated, may hold values from 0.5 to 1.5
- norm_bias: float32 [5, 768], replicated, may hold values from -1.8 to 1.8
- latents_cot: float32 [8, 128, 768], P('dp'), may hold values from -6 to 6
Outputs:
- latents_out: float32 [8, 128, 768], P('dp')
- grad_tokens: bfloat16 [8, 6312, 768], P('dp', 'head')
- grad_latents: float32 [8, 128, 768], P('dp')
- grad_cross_q: float32 [768, 768], P('head', 'dp')
- grad_cross_kv: float32 [2, 768, 768], P(None, 'head', 'dp')
- grad_cross_out: float32 [768, 768], P('head', 'dp')
- grad_cross_up: float32 [768, 3072], P('dp', 'head')
- grad_cross_down: float32 [3072, 768], P('head', 'dp')
- grad_self_qkv: float32 [3, 768, 768], P(None, 'head', 'dp')
- grad_self_out: float32 [768, 768], P('head', 'dp')
- grad_self_up: float32 [768, 3072], P('dp', 'head')
- grad_self_down: float32 [3072, 768], P('head', 'dp')
- grad_head_bias: float32 [2, 2, 768], P(None, None, 'head')
- grad_up_bias: float32 [2, 3072], P(None, 'head')
- grad_out_bias: float32 [2, 2, 768], P(None, None, 'head')
- grad_norm_gain: float32 [5, 768], P(None, 'head')
- grad_norm_bias: float32 [5, 768], P(None, 'head')
Inputs may be any that keep to these rules, and one draw needn't show every extreme that they name: The patches of frames at or after frames[c] are padding.
All inputs are finite; a program needn't handle non-finite values. No bound on the sum of `text_mask` on one device may be relied on, other than what follows from the above.
Results may differ from a plain program's by a relative error of at most 0.018.
Values may be sent and summed in bfloat16 or wider, within the bound.
A program may use at most 128 MiB of HBM per device.

v0:
```python
from functools import partial
import jax
import jax.numpy as jnp
from jax import lax
from jax.sharding import PartitionSpec as P

HD = 64
P_SIZE = 392
F_MAX = 16
EPSILON = 1e-05
NEGATIVE = -1e30


def normed(tensor, gain_row, shift_row):
    row_mean = jnp.mean(tensor, axis=-1, keepdims=True)
    centered = tensor - row_mean
    spread = jnp.mean(centered * centered, axis=-1, keepdims=True)
    return centered * lax.rsqrt(spread + EPSILON) * gain_row + shift_row


def share_of(tensor, head_index, head_width):
    return lax.dynamic_slice_in_dim(tensor, head_index * head_width, head_width, tensor.ndim - 1)


def split_heads(tensor, heads_here):
    return tensor.reshape(
        tensor.shape[0], tensor.shape[1], heads_here, tensor.shape[2] // heads_here
    )


def merge_heads(tensor):
    return tensor.reshape(tensor.shape[0], tensor.shape[1], tensor.shape[2] * tensor.shape[3])


def join_heads(partial_sum):
    return lax.psum(partial_sum.astype(jnp.bfloat16), "head").astype(jnp.float32)


def join_back(partial_sum):
    return lax.psum(partial_sum.astype(jnp.bfloat16), "head").astype(jnp.float32)


def scores_of(queries, key_rows, usable):
    scores = jnp.einsum("qhe,khe->hqk", queries, key_rows, preferred_element_type=jnp.float32)
    return jnp.where(usable[None, None, :], scores, NEGATIVE)


def attend_parts(parts):
    queries, key_rows, values, usable = parts
    scores = scores_of(queries, key_rows, usable)
    row_max = jnp.max(scores, axis=-1, keepdims=True)
    powers = jnp.exp(scores - row_max)
    totals = jnp.sum(powers, axis=-1, keepdims=True)
    chances = (powers / totals).astype(jnp.bfloat16)
    mixture = jnp.einsum("hqk,khe->qhe", chances, values, preferred_element_type=jnp.float32)
    return (mixture.astype(jnp.bfloat16), row_max, totals)


def back_parts(parts):
    queries, key_rows, values, usable, row_max, totals, grad_mix = parts
    scores = scores_of(queries, key_rows, usable)
    chances = jnp.exp(scores - row_max) / totals
    rounded = chances.astype(jnp.bfloat16)
    grad_values = jnp.einsum(
        "hqk,qhe->khe", rounded, grad_mix, preferred_element_type=jnp.float32
    ).astype(jnp.bfloat16)
    grad_chances = jnp.einsum("qhe,khe->hqk", grad_mix, values, preferred_element_type=jnp.float32)
    inner_sum = jnp.sum(chances * grad_chances, axis=-1, keepdims=True)
    grad_scores = (chances * (grad_chances - inner_sum)).astype(jnp.bfloat16)
    grad_queries = jnp.einsum(
        "hqk,khe->qhe", grad_scores, key_rows, preferred_element_type=jnp.float32
    ).astype(jnp.bfloat16)
    grad_keys = jnp.einsum(
        "hqk,qhe->khe", grad_scores, queries, preferred_element_type=jnp.float32
    ).astype(jnp.bfloat16)
    return (grad_queries, grad_keys, grad_values)


def feed_forward(tensor, gain_row, shift_row, weight_up, bias_up, weight_down):
    hidden = normed(tensor, gain_row, shift_row).astype(jnp.bfloat16)
    pre_act = (
        jnp.einsum("cnd,df->cnf", hidden, weight_up, preferred_element_type=jnp.float32) + bias_up
    )
    activation = jax.nn.gelu(pre_act, approximate=True).astype(jnp.bfloat16)
    partial_sum = jnp.einsum(
        "cnf,fd->cnd", activation, weight_down, preferred_element_type=jnp.float32
    )
    return (join_heads(partial_sum), (hidden, pre_act, activation))


def feed_back(tensor, gain_row, shift_row, weight_up, weight_down, saved_acts, grad_out):
    hidden, pre_act, activation = saved_acts
    grad_branch = grad_out.astype(jnp.bfloat16)
    grad_weight_down = jnp.einsum(
        "cnf,cnd->fd", activation, grad_branch, preferred_element_type=jnp.float32
    )
    grad_act = jnp.einsum(
        "cnd,fd->cnf", grad_branch, weight_down, preferred_element_type=jnp.float32
    )
    unused, gelu_pull = jax.vjp(partial(jax.nn.gelu, approximate=True), pre_act)
    grad_pre = gelu_pull(grad_act)[0].astype(jnp.bfloat16)
    grad_weight_up = jnp.einsum("cnd,cnf->df", hidden, grad_pre, preferred_element_type=jnp.float32)
    grad_bias_up = jnp.sum(grad_pre.astype(jnp.float32), axis=(0, 1))
    grad_hidden = join_back(
        jnp.einsum("cnf,df->cnd", grad_pre, weight_up, preferred_element_type=jnp.float32)
    )
    unused_too, norm_pull = jax.vjp(normed, tensor, gain_row, shift_row)
    grad_tensor, grad_gain, grad_shift = norm_pull(grad_hidden)
    return (grad_tensor, grad_weight_up, grad_bias_up, grad_weight_down, grad_gain, grad_shift)


def local(
    tokens,
    frames,
    text_mask,
    latents,
    cross_q,
    cross_kv,
    cross_out,
    cross_up,
    cross_down,
    self_qkv,
    self_out,
    self_up,
    self_down,
    head_bias,
    up_bias,
    out_bias,
    norm_gain,
    norm_bias,
    latents_cot,
):
    head_index = lax.axis_index("head")
    head_width = cross_q.shape[0]
    heads_here = head_width // HD
    scaling = HD ** (-0.5)
    clips_here = tokens.shape[0]
    rows_here = tokens.shape[1]
    length = rows_here * lax.axis_size("head")
    position = jnp.arange(length, dtype=jnp.int32)
    text_full = jnp.concatenate(
        [jnp.zeros((clips_here, F_MAX * P_SIZE), jnp.int32), text_mask], axis=1
    )
    usable = (position[None, :] < frames[:, None] * P_SIZE) | (text_full == 1)
    gathered, weights_whole = (
        lax.all_gather(tokens, "head", axis=1, tiled=True),
        lax.all_gather(cross_kv, "head", axis=1, tiled=True),
    )
    full_rows = gathered.astype(jnp.float32)
    row_mean = jnp.mean(full_rows, axis=-1, keepdims=True)
    centered = full_rows - row_mean
    inverse = lax.rsqrt(jnp.mean(centered * centered, axis=-1, keepdims=True) + EPSILON)
    inputs = (centered * inverse * norm_gain[0] + norm_bias[0]).astype(jnp.bfloat16)
    key_value = jnp.einsum("cld,kwd->clkw", inputs, cross_kv, preferred_element_type=jnp.float32)
    key_rows = key_value[:, :, 0].astype(jnp.bfloat16)
    cross_values = (key_value[:, :, 1] + head_bias[0, 1]).astype(jnp.bfloat16)
    start_state = latents.astype(jnp.float32)
    latent_norm = normed(start_state, norm_gain[1], norm_bias[1]).astype(jnp.bfloat16)
    cross_queries = (
        (
            jnp.einsum("cnd,wd->cnw", latent_norm, cross_q, preferred_element_type=jnp.float32)
            + head_bias[0, 0]
        )
        * scaling
    ).astype(jnp.bfloat16)
    cross_parts = (
        split_heads(cross_queries, heads_here),
        split_heads(key_rows, heads_here),
        split_heads(cross_values, heads_here),
        usable,
    )
    cross_mix, cross_max, cross_totals = lax.map(attend_parts, cross_parts)
    cross_flat = merge_heads(cross_mix)
    after_cross = (
        start_state
        + join_heads(
            jnp.einsum("cnw,wd->cnd", cross_flat, cross_out, preferred_element_type=jnp.float32)
        )
        + out_bias[0, 0]
    )
    cross_branch, cross_saved = feed_forward(
        after_cross, norm_gain[2], norm_bias[2], cross_up, up_bias[0], cross_down
    )
    after_mlp = after_cross + cross_branch + out_bias[0, 1]
    self_norm = normed(after_mlp, norm_gain[3], norm_bias[3]).astype(jnp.bfloat16)
    triple = jnp.einsum("cnd,kwd->cnkw", self_norm, self_qkv, preferred_element_type=jnp.float32)
    self_queries = ((triple[:, :, 0] + head_bias[1, 0]) * scaling).astype(jnp.bfloat16)
    self_keys = triple[:, :, 1].astype(jnp.bfloat16)
    self_values = (triple[:, :, 2] + head_bias[1, 1]).astype(jnp.bfloat16)
    everyone = jnp.ones((clips_here, self_keys.shape[1]), dtype=bool)
    self_parts = (
        split_heads(self_queries, heads_here),
        split_heads(self_keys, heads_here),
        split_heads(self_values, heads_here),
        everyone,
    )
    self_mix, self_max, self_totals = lax.map(attend_parts, self_parts)
    self_flat = merge_heads(self_mix)
    after_self = (
        after_mlp
        + join_heads(
            jnp.einsum("cnw,wd->cnd", self_flat, self_out, preferred_element_type=jnp.float32)
        )
        + out_bias[1, 0]
    )
    self_branch, self_saved = feed_forward(
        after_self, norm_gain[4], norm_bias[4], self_up, up_bias[1], self_down
    )
    latents_out = after_self + self_branch + out_bias[1, 1]
    bias_self_mlp = jnp.sum(latents_cot, axis=(0, 1))
    grad_ln_four, grad_self_up, upbias_self, grad_self_down, gain_four, shift_four = feed_back(
        after_self, norm_gain[4], norm_bias[4], self_up, self_down, self_saved, latents_cot
    )
    grad_state = latents_cot + grad_ln_four
    bias_self_attn = jnp.sum(grad_state, axis=(0, 1))
    grad_attn_in = grad_state.astype(jnp.bfloat16)
    grad_self_out = jnp.einsum(
        "cnw,cnd->wd", self_flat, grad_attn_in, preferred_element_type=jnp.float32
    )
    grad_mix = jnp.einsum(
        "cnd,wd->cnw", grad_attn_in, self_out, preferred_element_type=jnp.float32
    ).astype(jnp.bfloat16)
    self_grads = lax.map(
        back_parts, self_parts + (self_max, self_totals, split_heads(grad_mix, heads_here))
    )
    grad_query_scaled = (merge_heads(self_grads[0]).astype(jnp.float32) * scaling).astype(
        jnp.bfloat16
    )
    grad_triple = jnp.stack(
        [grad_query_scaled, merge_heads(self_grads[1]), merge_heads(self_grads[2])], axis=2
    )
    grad_self_qkv = jnp.einsum(
        "cnd,cnkw->kwd", self_norm, grad_triple, preferred_element_type=jnp.float32
    )
    bias_self_q = jnp.sum(grad_triple[:, :, 0].astype(jnp.float32), axis=(0, 1))
    bias_self_v = jnp.sum(grad_triple[:, :, 2].astype(jnp.float32), axis=(0, 1))
    grad_self_in = join_back(
        jnp.einsum("cnkw,kwd->cnd", grad_triple, self_qkv, preferred_element_type=jnp.float32)
    )
    unused, norm_pull = jax.vjp(normed, after_mlp, norm_gain[3], norm_bias[3])
    grad_ln_three, gain_three, shift_three = norm_pull(grad_self_in)
    grad_state = grad_state + grad_ln_three
    bias_cross_mlp = jnp.sum(grad_state, axis=(0, 1))
    grad_ln_two, grad_cross_up, upbias_cross, grad_cross_down, gain_two, shift_two = feed_back(
        after_cross, norm_gain[2], norm_bias[2], cross_up, cross_down, cross_saved, grad_state
    )
    grad_state = grad_state + grad_ln_two
    bias_cross_attn = jnp.sum(grad_state, axis=(0, 1))
    grad_attn_in = grad_state.astype(jnp.bfloat16)
    grad_cross_out = jnp.einsum(
        "cnw,cnd->wd", cross_flat, grad_attn_in, preferred_element_type=jnp.float32
    )
    grad_mix = jnp.einsum(
        "cnd,wd->cnw", grad_attn_in, cross_out, preferred_element_type=jnp.float32
    ).astype(jnp.bfloat16)
    cross_grads = lax.map(
        back_parts, cross_parts + (cross_max, cross_totals, split_heads(grad_mix, heads_here))
    )
    grad_query_cross = (merge_heads(cross_grads[0]).astype(jnp.float32) * scaling).astype(
        jnp.bfloat16
    )
    grad_cross_q = jnp.einsum(
        "cnd,cnw->wd", latent_norm, grad_query_cross, preferred_element_type=jnp.float32
    )
    bias_cross_q = jnp.sum(grad_query_cross.astype(jnp.float32), axis=(0, 1))
    grad_latent_in = join_back(
        jnp.einsum("cnw,wd->cnd", grad_query_cross, cross_q, preferred_element_type=jnp.float32)
    )
    unused_too, latent_pull = jax.vjp(normed, start_state, norm_gain[1], norm_bias[1])
    grad_ln_one, gain_one, shift_one = latent_pull(grad_latent_in)
    grad_latents = grad_state + grad_ln_one
    grad_pair = jnp.stack([merge_heads(cross_grads[1]), merge_heads(cross_grads[2])], axis=2)
    grad_cross_kv = jnp.einsum(
        "cld,clkw->kwd", inputs, grad_pair, preferred_element_type=jnp.float32
    )
    bias_cross_v = jnp.sum(grad_pair[:, :, 1].astype(jnp.float32), axis=(0, 1))
    arrived = lax.all_to_all(grad_pair, "head", split_axis=1, concat_axis=3, tiled=True)
    grad_share = jnp.einsum(
        "clkw,kwd->cld", arrived, weights_whole, preferred_element_type=jnp.float32
    )
    own_start = head_index * rows_here
    own_mean = lax.dynamic_slice_in_dim(row_mean, own_start, rows_here, 1)
    own_inverse = lax.dynamic_slice_in_dim(inverse, own_start, rows_here, 1)
    standard = (tokens.astype(jnp.float32) - own_mean) * own_inverse
    scaled = grad_share * norm_gain[0]
    mean_plain = jnp.mean(scaled, axis=-1, keepdims=True)
    mean_cross = jnp.mean(scaled * standard, axis=-1, keepdims=True)
    grad_tokens = (own_inverse * (scaled - mean_plain - standard * mean_cross)).astype(jnp.bfloat16)
    gain_zero, shift_zero = lax.psum(
        (jnp.sum(grad_share * standard, axis=(0, 1)), jnp.sum(grad_share, axis=(0, 1))), "head"
    )
    grad_head_bias = jnp.stack(
        [jnp.stack([bias_cross_q, bias_cross_v]), jnp.stack([bias_self_q, bias_self_v])]
    )
    grad_up_bias = jnp.stack([upbias_cross, upbias_self])
    out_full = jnp.stack(
        [jnp.stack([bias_cross_attn, bias_cross_mlp]), jnp.stack([bias_self_attn, bias_self_mlp])]
    )
    grad_out_bias = share_of(out_full, head_index, head_width)
    grad_norm_gain = share_of(
        jnp.stack([gain_zero, gain_one, gain_two, gain_three, gain_four]), head_index, head_width
    )
    grad_norm_bias = share_of(
        jnp.stack([shift_zero, shift_one, shift_two, shift_three, shift_four]),
        head_index,
        head_width,
    )
    small_sums = lax.psum(
        (grad_head_bias, grad_up_bias, grad_out_bias, grad_norm_gain, grad_norm_bias), "dp"
    )
    combined = (
        lax.psum_scatter(grad_cross_q, "dp", scatter_dimension=1, tiled=True),
        lax.psum_scatter(grad_cross_kv, "dp", scatter_dimension=2, tiled=True),
        lax.psum_scatter(grad_cross_out, "dp", scatter_dimension=1, tiled=True),
        lax.psum_scatter(grad_cross_up, "dp", scatter_dimension=0, tiled=True),
        lax.psum_scatter(grad_cross_down, "dp", scatter_dimension=1, tiled=True),
        lax.psum_scatter(grad_self_qkv, "dp", scatter_dimension=2, tiled=True),
        lax.psum_scatter(grad_self_out, "dp", scatter_dimension=1, tiled=True),
        lax.psum_scatter(grad_self_up, "dp", scatter_dimension=0, tiled=True),
        lax.psum_scatter(grad_self_down, "dp", scatter_dimension=1, tiled=True),
    )
    cross_sums = combined[:5]
    self_sums = combined[5:]
    return (
        latents_out,
        grad_tokens,
        grad_latents,
        cross_sums[0],
        cross_sums[1],
        cross_sums[2],
        cross_sums[3],
        cross_sums[4],
        self_sums[0],
        self_sums[1],
        self_sums[2],
        self_sums[3],
        small_sums[0],
        small_sums[1],
        small_sums[2],
        small_sums[3],
        small_sums[4],
    )


def solution(mesh):
    in_specs = (
        P("dp", "head", None),
        P("dp"),
        P("dp", None),
        P("dp", None, None),
        P("head", None),
        P(None, "head", None),
        P("head", None),
        P(None, "head"),
        P("head", None),
        P(None, "head", None),
        P("head", None),
        P(None, "head"),
        P("head", None),
        P(None, None, "head"),
        P(None, "head"),
        P(),
        P(),
        P(),
        P("dp", None, None),
    )
    out_specs = (
        P("dp", None, None),
        P("dp", "head", None),
        P("dp", None, None),
        P("head", "dp"),
        P(None, "head", "dp"),
        P("head", "dp"),
        P("dp", "head"),
        P("head", "dp"),
        P(None, "head", "dp"),
        P("head", "dp"),
        P("dp", "head"),
        P("head", "dp"),
        P(None, None, "head"),
        P(None, "head"),
        P(None, None, "head"),
        P(None, "head"),
        P(None, "head"),
    )
    return jax.shard_map(local, mesh=mesh, in_specs=in_specs, out_specs=out_specs, check_vma=False)
```

profile of v0, /device:TPU:0, one launch (start us, length us, event | category | flops | bytes accessed | tf_op | source)
XLA Modules:
  0.0 1166.3 jit_solution(2360226538765348507)
XLA Ops:
  7.3 18.4 %copy.55 = bf16[1,1578,768]{2,0,1:T(2,128)(2,1)} copy(bf16[1,1578,768]{2,1,0:T(8,128)(2,1)} %param.19) | data formatting | bytes 4847616 | tf_op args[0]
  28.8 122.7 %all-gather.3.cloned.1.call-done = bf16[1,6312,768]{2,0,1:T(2,128)(2,1)} async-done(((bf16[1,1578,768]{2,0,1:T(2,128)(2,1)}), bf16[1,6312,768]{2,0,1:T(2,128)(2,1)}) %all-gather.3.cloned.1.call-update) | async-done | bytes 9695248 | tf_op jit(solution)/shard_map/all_gather | solution.py:146
  159.0 14.1 %fusion.4 = f32[6312]{0:T(1024)S(1)} fusion(f32[6312]{0:T(1024)S(1)} %broadcast_multiply_fusion, bf16[1,6312,768]{2,0,1:T(2,128)(2,1)} %all-gather.3.cloned.1.call-done), kind=kLoop, calls=%fused_computation.6 | loop fusion | flops 19384152 | bytes 9745728 | tf_op jit(solution)/shard_map/reduce_sum | solution.py:152
  201.4 31.3 %all-reduce.12.cloned.1.call-done = bf16[1,128,768]{2,1,0:T(8,128)(2,1)} async-done(((bf16[1,128,768]{2,1,0:T(8,128)(2,1)}), bf16[1,128,768]{2,1,0:T(8,128)(2,1)}) %all-reduce.12.cloned.1.call-update) | async-done | bytes 196624 | tf_op jit(solution)/shard_map/psum | solution.py:36
  239.6 30.8 %all-reduce.14.cloned.1.call-done = bf16[1,128,768]{2,1,0:T(8,128)(2,1)} async-done(((bf16[1,128,768]{2,1,0:T(8,128)(2,1)}), bf16[1,128,768]{2,1,0:T(8,128)(2,1)}) %all-reduce.14.cloned.1.call-update) | async-done | bytes 196624 | tf_op jit(solution)/shard_map/psum | solution.py:36
  280.2 32.1 %all-reduce.16.cloned.1.call-done = bf16[1,128,768]{2,1,0:T(8,128)(2,1)} async-done(((bf16[1,128,768]{2,1,0:T(8,128)(2,1)}), bf16[1,128,768]{2,1,0:T(8,128)(2,1)}) %all-reduce.16.cloned.1.call-update) | async-done | bytes 196624 | tf_op jit(solution)/shard_map/psum | solution.py:36
  320.6 32.1 %all-reduce.18.cloned.1.call-done = bf16[1,128,768]{2,1,0:T(8,128)(2,1)} async-done(((bf16[1,128,768]{2,1,0:T(8,128)(2,1)}), bf16[1,128,768]{2,1,0:T(8,128)(2,1)}) %all-reduce.18.cloned.1.call-update) | async-done | bytes 196624 | tf_op jit(solution)/shard_map/psum | solution.py:40
  369.2 32.1 %all-reduce.20.cloned.1.call-done = bf16[1,128,768]{2,1,0:T(8,128)(2,1)} async-done(((bf16[1,128,768]{2,1,0:T(8,128)(2,1)}), bf16[1,128,768]{2,1,0:T(8,128)(2,1)}) %all-reduce.20.cloned.1.call-update) | async-done | bytes 196624 | tf_op jit(solution)/shard_map/psum | solution.py:40
  412.8 29.3 %all-reduce.22.cloned.1.call-done = bf16[1,128,768]{2,1,0:T(8,128)(2,1)} async-done(((bf16[1,128,768]{2,1,0:T(8,128)(2,1)}), bf16[1,128,768]{2,1,0:T(8,128)(2,1)}) %all-reduce.22.cloned.1.call-update) | async-done | bytes 196624 | tf_op jit(solution)/shard_map/psum | solution.py:40
  447.5 11.8 %multiply_reduce_fusion = (f32[3,128]{1,0:T(4,128)S(1)}, f32[3,128,6312]{1,2,0:T(8,128)}) fusion(f32[3,128,6312]{1,2,0:T(8,128)} %get-tuple-element.188, f32[3,128]{1,0:T(4,128)S(1)} %copy-done.84, bf16[128,3,64]{0,2,1:T(8,128)(2,1)S(1)} %bitcast.256, f32[6312,3,64]{0,2,1:T(8,128)} %bitcast.227, f32[3,64]{1,0:T(4,128)S(1)} %copy-done.93), kind=kOutput, calls=%fused_computation.16 | convolution fusion | flops 319942272 | bytes 24291072 | tf_op jit(solution)/shard_map/while/body/eval_jaxpr/qhe,khe->hqk/dot_general | solution.py:67
  459.3 9.9 multiply_convert_fusion
  529.6 16.4 %copy.61 = bf16[1,6312,2,192]{3,2,0,1:T(2,128)(2,1)} copy(bf16[1,6312,2,192]{1,3,2,0:T(8,128)(2,1)} %pad_maximum_fusion) | data formatting | bytes 9695232 | tf_op jit(solution)/shard_map/stack | solution.py:272
  560.5 13.6 %reduce-scatter.36.cloned.1.call-done = f32[96,192]{1,0:T(8,128)} async-done(((f32[768,192]{1,0:T(8,128)}), f32[96,192]{1,0:T(8,128)}) %reduce-scatter.36.cloned.1.call-update) | async-done | bytes 73744
  575.7 63.7 %reduce-scatter.28.cloned.1.call-done = f32[96,192]{1,0:T(8,128)} async-done(((f32[768,192]{1,0:T(8,128)}), f32[96,192]{1,0:T(8,128)}) %reduce-scatter.28.cloned.1.call-update) | async-done | bytes 73744
  641.1 64.0 %reduce-scatter.32.cloned.1.call-done = f32[96,192]{1,0:T(8,128)} async-done(((f32[768,192]{1,0:T(8,128)}), f32[96,192]{1,0:T(8,128)}) %reduce-scatter.32.cloned.1.call-update) | async-done | bytes 73744
  706.7 65.4 %reduce-scatter.30.cloned.1.call-done = f32[96,384]{1,0:T(8,128)} async-done(((f32[768,384]{1,0:T(8,128)}), f32[96,384]{1,0:T(8,128)}) %reduce-scatter.30.cloned.1.call-update) | async-done | bytes 147472
  774.0 68.6 %reduce-scatter.34.cloned.1.call-done = f32[96,576]{1,0:T(8,128)} async-done(((f32[768,576]{1,0:T(8,128)}), f32[96,576]{1,0:T(8,128)}) %reduce-scatter.34.cloned.1.call-update) | async-done | bytes 221200
  844.6 17.2 %copy.62 = bf16[1,4,1578,2,192]{2,4,1,3,0:T(8,128)(2,1)} copy(bf16[1,4,1578,2,192]{4,3,2,1,0:T(2,128)(2,1)} %bitcast.46) | data formatting | bytes 9695232 | tf_op jit(solution)/shard_map/all_to_all | solution.py:277
  867.0 9.0 fusion.13
  885.4 37.7 %all-reduce.1 = (f32[2,2,192]{2,1,0:T(2,128)}, f32[2,768]{1,0:T(2,128)}, f32[2,2,192]{2,1,0:T(2,128)}, f32[5,192]{1,0:T(8,128)}, f32[5,192]{1,0:T(8,128)}) all-reduce(f32[2,2,192]{2,1,0:T(2,128)S(1)} %pad_maximum_fusion.2, f32[2,768]{1,0:T(2,128)S(1)} %pad_maximum_fusion.1, ...), channel_id=1, replica_groups=mesh['dp'=8,'head'=4] {'dp'}, use_global_device_ids=true, to_apply=%region_47.48 | all-reduce | flops 4992 | bytes 39936 | tf_op jit(solution)/shard_map/psum | solution.py:308
  928.4 12.5 %reduce-scatter.24.cloned.1.call-done = f32[96,768]{1,0:T(8,128)} async-done(((f32[768,768]{1,0:T(8,128)}), f32[96,768]{1,0:T(8,128)}) %reduce-scatter.24.cloned.1.call-update) | async-done | bytes 294928 | tf_op jit(solution)/shard_map/reduce_scatter | solution.py:319
  940.9 72.7 %reduce-scatter.26.cloned.1.call-done = f32[768,96]{0,1:T(8,128)} async-done(((f32[768,768]{0,1:T(8,128)}), f32[768,96]{0,1:T(8,128)}) %reduce-scatter.26.cloned.1.call-update) | async-done | bytes 294928 | tf_op jit(solution)/shard_map/reduce_scatter | solution.py:320
  1013.6 72.9 %reduce-scatter.20.cloned.1.call-done = f32[96,768]{1,0:T(8,128)} async-done(((f32[768,768]{1,0:T(8,128)}), f32[96,768]{1,0:T(8,128)}) %reduce-scatter.20.cloned.1.call-update) | async-done | bytes 294928 | tf_op jit(solution)/shard_map/reduce_scatter | solution.py:315
  1086.5 72.8 %reduce-scatter.22.cloned.1.call-done = f32[768,96]{0,1:T(8,128)} async-done(((f32[768,768]{0,1:T(8,128)}), f32[768,96]{0,1:T(8,128)}) %reduce-scatter.22.cloned.1.call-update) | async-done | bytes 294928 | tf_op jit(solution)/shard_map/reduce_scatter | solution.py:316
  (381 shorter events, 198.4 us)
Async XLA Ops:
  7.2 229.9 %copy-start = (bf16[768,768]{1,0:T(8,128)(2,1)S(1)}, bf16[768,768]{1,0:T(8,128)(2,1)}, u32[]{:S(2)}) copy-start(bf16[768,768]{1,0:T(8,128)(2,1)} %param.27) | copy-start | bytes 3538948
  7.3 144.2 %all-gather.3.cloned.1.call-start = ((), (), s32[]{:S(2)}) async-start(), calls=%async_computation.10 | async-start | bytes 24238080 | tf_op jit(solution)/shard_map/all_gather | solution.py:146
  25.7 207.0 %all-reduce.12.cloned.1.call-start = ((), (), s32[]{:S(2)}) async-start(), calls=%async_computation.11 | async-start | bytes 393216 | tf_op jit(solution)/shard_map/psum | solution.py:36
  25.9 168.6 %copy-start.92 = (f32[3,64]{1,0:T(4,128)}, f32[3,64]{1,0:T(4,128)S(1)}, u32[]{:S(2)}) copy-start(f32[3,64]{1,0:T(4,128)S(1)} %add.344) | copy-start | bytes 2308
  27.9 207.1 %copy-start.47 = (f32[768]{0:T(1024)}, f32[768]{0:T(1024)S(1)}, u32[]{:S(2)}) copy-start(f32[768]{0:T(1024)S(1)} %get-tuple-element.151) | copy-start | bytes 9220
  28.7 154.8 %copy-start.35 = (bf16[128,192]{0,1:T(8,128)(2,1)}, bf16[128,192]{0,1:T(8,128)(2,1)S(1)}, u32[]{:S(2)}) copy-start(bf16[128,192]{0,1:T(8,128)(2,1)S(1)} %fusion.33) | copy-start | bytes 147460
  200.6 69.8 %all-reduce.14.cloned.1.call-start = ((), (), s32[]{:S(2)}) async-start(), calls=%async_computation.12 | async-start | bytes 393216 | tf_op jit(solution)/shard_map/psum | solution.py:36
  238.2 74.1 %all-reduce.16.cloned.1.call-start = ((), (), s32[]{:S(2)}) async-start(), calls=%async_computation.13 | async-start | bytes 393216 | tf_op jit(solution)/shard_map/psum | solution.py:36
  280.1 72.6 %all-reduce.18.cloned.1.call-start = ((), (), s32[]{:S(2)}) async-start(), calls=%async_computation.14 | async-start | bytes 393216 | tf_op jit(solution)/shard_map/psum | solution.py:40
  320.6 80.8 %all-reduce.20.cloned.1.call-start = ((), (), s32[]{:S(2)}) async-start(), calls=%async_computation.15 | async-start | bytes 393216 | tf_op jit(solution)/shard_map/psum | solution.py:40
  369.1 72.9 %all-reduce.22.cloned.1.call-start = ((), (), s32[]{:S(2)}) async-start(), calls=%async_computation.16 | async-start | bytes 393216 | tf_op jit(solution)/shard_map/psum | solution.py:40
  409.9 146.2 %all-reduce.24.cloned.1.call-start = ((), (), s32[]{:S(2)}) async-start(), calls=%async_computation.27 | async-start | bytes 786432 | tf_op jit(solution)/shard_map/psum | solution.py:36
  474.5 99.6 %reduce-scatter.36.cloned.1.call-start = ((), (), s32[]{:S(2)}) async-start(), calls=%async_computation.26 | async-start | bytes 884736
  475.8 163.7 %reduce-scatter.28.cloned.1.call-start = ((), (), s32[]{:S(2)}) async-start(), calls=%async_computation.22 | async-start | bytes 884736
  478.4 226.7 %reduce-scatter.32.cloned.1.call-start = ((), (), s32[]{:S(2)}) async-start(), calls=%async_computation.24 | async-start | bytes 884736
  485.4 286.7 %reduce-scatter.30.cloned.1.call-start = ((), (), s32[]{:S(2)}) async-start(), calls=%async_computation.23 | async-start | bytes 1327104
  506.9 335.6 %reduce-scatter.34.cloned.1.call-start = ((), (), s32[]{:S(2)}) async-start(), calls=%async_computation.25 | async-start | bytes 2211840
  517.7 349.4 %all-gather.5.cloned.1.call-start = ((), (), s32[]{:S(2)}) async-start(), calls=%async_computation.17 | async-start | bytes 2949120 | tf_op jit(solution)/shard_map/all_gather | solution.py:147
  518.3 422.6 %reduce-scatter.24.cloned.1.call-start = ((), (), s32[]{:S(2)}) async-start(), calls=%async_computation.20 | async-start | bytes 2654208 | tf_op jit(solution)/shard_map/reduce_scatter | solution.py:319
  520.4 493.2 %reduce-scatter.26.cloned.1.call-start = ((), (), s32[]{:S(2)}) async-start(), calls=%async_computation.21 | async-start | bytes 2654208 | tf_op jit(solution)/shard_map/reduce_scatter | solution.py:320
  522.4 564.1 %reduce-scatter.20.cloned.1.call-start = ((), (), s32[]{:S(2)}) async-start(), calls=%async_computation.18 | async-start | bytes 2654208 | tf_op jit(solution)/shard_map/reduce_scatter | solution.py:315
  546.1 298.5 %all-to-all-start = ((bf16[1,6312,2,192]{3,2,0,1:T(2,128)(2,1)}), bf16[1,6312,2,192]{3,2,0,1:T(2,128)(2,1)}, u32[]{:S(2)}, u32[]{:S(2)}) async-start(bf16[1,6312,2,192]{3,2,0,1:T(2,128)(2,1)} %copy.61), calls=%async_computation | async-start | bytes 12926976 | tf_op jit(solution)/shard_map/all_to_all | solution.py:277
  551.5 607.7 %reduce-scatter.22.cloned.1.call-start = ((), (), s32[]{:S(2)}) async-start(), calls=%async_computation.19 | async-start | bytes 2654208 | tf_op jit(solution)/shard_map/reduce_scatter | solution.py:316
  923.1 236.1 %copy-start.1 = (bf16[768,768]{1,0:T(8,128)(2,1)S(1)}, bf16[768,768]{1,0:T(8,128)(2,1)}, u32[]{:S(2)}) copy-start(bf16[768,768]{1,0:T(8,128)(2,1)} %param.27) | copy-start | bytes 3538948
  (96 other events, 2352.8 us)
Sparse Core Ops, SparseCore 0:
  25.9 125.5 all-gather.2
  200.7 31.9 all-reduce.11
  238.3 32.0 all-reduce.13
  280.2 32.0 all-reduce.15
  320.7 32.0 all-reduce.17
  369.2 32.0 all-reduce.19
  410.0 32.0 all-reduce.21
  474.6 32.8 all-reduce.23
  510.8 63.2 reduce-scatter.35
  577.3 62.1 reduce-scatter.27
  642.8 62.2 reduce-scatter.31
  708.3 63.7 reduce-scatter.29
  776.1 66.3 reduce-scatter.33
  844.0 22.9 all-gather.4
  870.9 69.9 reduce-scatter.23
  944.8 68.7 reduce-scatter.25
  1017.5 68.9 reduce-scatter.19
  1090.4 68.7 reduce-scatter.21
where the time goes:
time: 1170 us
  waiting for transfers between devices  823 us (70%)
  matrix products  102 us (9%)
  local copies, waits for them, and re-layouts  92.2 us (8%)
  other arithmetic  81.6 us (7%)
  blocking collectives  44.1 us (4%)
  between operations  16.7 us (1%)
    unnamed x23, waiting for transfers between devices  276 us
    all_gather x1, waiting for transfers between devices, local(): lax.all_gather(tokens, 'head', axis=1, tiled=True)  123 us
    psum x4, waiting for transfers between devices, join_heads(): lax.psum(partial_sum.astype(jnp.bfloat16), 'head').astype(jnp.float32)  94.2 us
    psum x3, waiting for transfers between devices, join_back(): lax.psum(partial_sum.astype(jnp.bfloat16), 'head').astype(jnp.float32)  93.6 us
    reduce_scatter x1, waiting for transfers between devices, local(): lax.psum_scatter(grad_cross_up, 'dp', scatter_dimension=0, tiled=True)  72.9 us
    reduce_scatter x1, waiting for transfers between devices, local(): lax.psum_scatter(grad_cross_down, 'dp', scatter_dimension=1, tiled=True)  72.8 us
    reduce_scatter x1, waiting for transfers between devices, local(): lax.psum_scatter(grad_self_down, 'dp', scatter_dimension=1, tiled=True)  72.7 us
    unnamed x214, local copies, waits for them, and re-layouts  51.9 us
  transfers between devices with their start and end apart: 19, of which 17 were waited for; matrix products, arithmetic and copies ran while one was open for 11% of the time, Pallas kernels for 0%

commit v1 on v0

--- a/solution.py
+++ b/solution.py
@@ -9,6 +9,27 @@
 F_MAX = 16
 EPSILON = 1e-05
 NEGATIVE = -1e30
+
+
+def collect(array, axis, dim):
+    count, mine, rows = (lax.axis_size(axis), lax.axis_index(axis), array.shape[dim])
+    ahead = [(i, (i + 1) % count) for i in range(count)]
+    left = [(i, (i - 1) % count) for i in range(count)]
+    out = jnp.zeros((*array.shape[:dim], count * rows, *array.shape[dim + 1 :]), array.dtype)
+    out = lax.dynamic_update_slice_in_dim(out, array, mine * rows, axis=dim)
+    from_left = from_right = array
+    half = count // 2
+    for step in range(1, half + 1):
+        from_left = lax.ppermute(from_left, axis, ahead)
+        out = lax.dynamic_update_slice_in_dim(
+            out, from_left, (mine - step) % count * rows, axis=dim
+        )
+        if step < count - half:
+            from_right = lax.ppermute(from_right, axis, left)
+            out = lax.dynamic_update_slice_in_dim(
+                out, from_right, (mine + step) % count * rows, axis=dim
+            )
+    return out
 
 
 def normed(tensor, gain_row, shift_row):
@@ -143,7 +164,7 @@
     )
     usable = (position[None, :] < frames[:, None] * P_SIZE) | (text_full == 1)
     gathered, weights_whole = (
-        lax.all_gather(tokens, "head", axis=1, tiled=True),
+        collect(tokens, "head", 1),
         lax.all_gather(cross_kv, "head", axis=1, tiled=True),
     )
     full_rows = gathered.astype(jnp.float32)

time: 1170 us -> 1130 us (0.966)
  waiting for transfers between devices: 823 us -> 751 us
  local copies, waits for them, and re-layouts: 92.2 us -> 128 us
  other arithmetic: 81.6 us -> 64.9 us
    all_gather x1 -> x0, waiting for transfers between devices: 123 us -> none  [local(): lax.all_gather(tokens, 'head', axis=1, tiled=True)]
    ppermute x0 -> x3, waiting for transfers between devices: none -> 51 us  [the longest x2 51 us: collect(): from_left = lax.ppermute(from_left, axis, ahead)]
    dynamic_update_slice x0 -> x4, local copies, waits for them, and re-layouts: none -> 50 us  [the longest x2 24.7 us: collect(): lax.dynamic_update_slice_in_dim(out, from_left, (mine - step) % count * r...]
    unnamed x214 -> x215, local copies, waits for them, and re-layouts: 51.9 us -> 33.9 us
    unnamed x23 -> x22, waiting for transfers between devices: 276 us -> 274 us
  transfers between devices with their start and end apart: 19 -> 21, of which waited for: 17 -> 17; matrix products, arithmetic and copies ran while one was open for 11% -> 15% of each run, Pallas kernels for 0% -> 0%
where the time goes in v1:
time: 1130 us; the launch traced here: 1120 us
  waiting for transfers between devices  751 us (66%)
  local copies, waits for them, and re-layouts  128 us (11%)
  matrix products  108 us (10%)
  other arithmetic  64.9 us (6%)
  blocking collectives  44.2 us (4%)
  between operations  16.3 us (1%)
  starting transfers between devices  12 us (1%)
    unnamed x22, waiting for transfers between devices  274 us
    psum x4, waiting for transfers between devices, join_heads(): lax.psum(partial_sum.astype(jnp.bfloat16), 'head').astype(jnp.float32)  95.9 us
    psum x3, waiting for transfers between devices, join_back(): lax.psum(partial_sum.astype(jnp.bfloat16), 'head').astype(jnp.float32)  93.6 us
    reduce_scatter x1, waiting for transfers between devices, local(): lax.psum_scatter(grad_cross_up, 'dp', scatter_dimension=0, tiled=True)  73 us
    reduce_scatter x1, waiting for transfers between devices, local(): lax.psum_scatter(grad_cross_down, 'dp', scatter_dimension=1, tiled=True)  72.9 us
    reduce_scatter x1, waiting for transfers between devices, local(): lax.psum_scatter(grad_self_down, 'dp', scatter_dimension=1, tiled=True)  72.9 us
    ppermute x2, waiting for transfers between devices, collect(): from_left = lax.ppermute(from_left, axis, ahead)  51 us
    psum x1, blocking collectives, local(): lax.psum((grad_head_bias, grad_up_bias, grad_out_bias, grad_norm_gain, gr...  37.9 us
  transfers between devices with their start and end apart: 21, of which 17 were waited for; matrix products, arithmetic and copies ran while one was open for 15% of the time, Pallas kernels for 0%

profile of v1, /device:TPU:0, one launch (start us, length us, event | category | flops | bytes accessed | tf_op | source)
XLA Modules:
  0.0 1123.8 jit_solution(12260332321112959065)
XLA Ops:
  9.8 51.0 %collective-permute-done = bf16[1,1578,768]{2,1,0:T(8,128)(2,1)} collective-permute-done((bf16[1,1578,768]{2,1,0:T(8,128)(2,1)}, bf16[1,1578,768]{2,1,0:T(8,128)(2,1)}, u32[]{:S(2)}, u32[]{:S(2)}) %collective-permute-start) | collective-permute-done | bytes 2423840 | tf_op jit(solution)/shard_map/ppermute | solution.py:23
  69.2 12.7 %dynamic_update_slice.39 = bf16[1,6312,768]{2,1,0:T(8,128)(2,1)} dynamic-update-slice(bf16[1,6312,768]{2,1,0:T(8,128)(2,1)} %broadcast_in_dim.155, bf16[1,1578,768]{2,1,0:T(8,128)(2,1)} %param.19, s32[]{:T(128)} %constant.158.clone.1, s32[]{:T(128)S(6)} %select_n.46, s32[]{:T(128)} %constant.158.clone.1) | dynamic-update-slice | bytes 4847620 | tf_op jit(solution)/shard_map/dynamic_update_slice | solution.py:19
  84.1 12.1 %dynamic_update_slice.40 = bf16[1,6312,768]{2,1,0:T(8,128)(2,1)} dynamic-update-slice(bf16[1,6312,768]{2,1,0:T(8,128)(2,1)} %dynamic_update_slice.39, bf16[1,1578,768]{2,1,0:T(8,128)(2,1)} %collective-permute-done, s32[]{:T(128)} %constant.158.clone.1, s32[]{:T(128)S(6)} %select_n.48, s32[]{:T(128)} %constant.158.clone.1) | dynamic-update-slice | bytes 4847620 | tf_op jit(solution)/shard_map/dynamic_update_slice | solution.py:24
  96.1 12.6 %dynamic_update_slice.41 = bf16[1,6312,768]{2,1,0:T(8,128)(2,1)} dynamic-update-slice(bf16[1,6312,768]{2,1,0:T(8,128)(2,1)} %dynamic_update_slice.40, bf16[1,1578,768]{2,1,0:T(8,128)(2,1)} %collective-permute-done.1, s32[]{:T(128)} %constant.158.clone.1, s32[]{:T(128)S(6)} %select_n.50, s32[]{:T(128)} %constant.158.clone.1) | dynamic-update-slice | bytes 4847620 | tf_op jit(solution)/shard_map/dynamic_update_slice | solution.py:29
  108.7 12.6 %dynamic_update_slice.42 = bf16[1,6312,768]{2,1,0:T(8,128)(2,1)} dynamic-update-slice(bf16[1,6312,768]{2,1,0:T(8,128)(2,1)} %dynamic_update_slice.41, bf16[1,1578,768]{2,1,0:T(8,128)(2,1)} %collective-permute-done.2, s32[]{:T(128)} %constant.158.clone.1, s32[]{:T(128)S(6)} %select_n.52, s32[]{:T(128)} %constant.158.clone.1) | dynamic-update-slice | bytes 4847620 | tf_op jit(solution)/shard_map/dynamic_update_slice | solution.py:24
  156.7 33.0 %all-reduce.12.cloned.1.call-done = bf16[1,128,768]{2,1,0:T(8,128)(2,1)} async-done(((bf16[1,128,768]{2,1,0:T(8,128)(2,1)}), bf16[1,128,768]{2,1,0:T(8,128)(2,1)}) %all-reduce.12.cloned.1.call-update) | async-done | bytes 196624 | tf_op jit(solution)/shard_map/psum | solution.py:57
  196.5 30.8 %all-reduce.14.cloned.1.call-done = bf16[1,128,768]{2,1,0:T(8,128)(2,1)} async-done(((bf16[1,128,768]{2,1,0:T(8,128)(2,1)}), bf16[1,128,768]{2,1,0:T(8,128)(2,1)}) %all-reduce.14.cloned.1.call-update) | async-done | bytes 196624 | tf_op jit(solution)/shard_map/psum | solution.py:57
  237.1 32.1 %all-reduce.16.cloned.1.call-done = bf16[1,128,768]{2,1,0:T(8,128)(2,1)} async-done(((bf16[1,128,768]{2,1,0:T(8,128)(2,1)}), bf16[1,128,768]{2,1,0:T(8,128)(2,1)}) %all-reduce.16.cloned.1.call-update) | async-done | bytes 196624 | tf_op jit(solution)/shard_map/psum | solution.py:57
  277.5 32.1 %all-reduce.18.cloned.1.call-done = bf16[1,128,768]{2,1,0:T(8,128)(2,1)} async-done(((bf16[1,128,768]{2,1,0:T(8,128)(2,1)}), bf16[1,128,768]{2,1,0:T(8,128)(2,1)}) %all-reduce.18.cloned.1.call-update) | async-done | bytes 196624 | tf_op jit(solution)/shard_map/psum | solution.py:61
  326.1 32.1 %all-reduce.20.cloned.1.call-done = bf16[1,128,768]{2,1,0:T(8,128)(2,1)} async-done(((bf16[1,128,768]{2,1,0:T(8,128)(2,1)}), bf16[1,128,768]{2,1,0:T(8,128)(2,1)}) %all-reduce.20.cloned.1.call-update) | async-done | bytes 196624 | tf_op jit(solution)/shard_map/psum | solution.py:61
  369.7 29.3 %all-reduce.22.cloned.1.call-done = bf16[1,128,768]{2,1,0:T(8,128)(2,1)} async-done(((bf16[1,128,768]{2,1,0:T(8,128)(2,1)}), bf16[1,128,768]{2,1,0:T(8,128)(2,1)}) %all-reduce.22.cloned.1.call-update) | async-done | bytes 196624 | tf_op jit(solution)/shard_map/psum | solution.py:61
  404.4 11.8 %multiply_reduce_fusion = (f32[3,128]{1,0:T(4,128)S(1)}, f32[3,128,6312]{1,2,0:T(8,128)}) fusion(f32[3,128,6312]{1,2,0:T(8,128)} %get-tuple-element.188, f32[3,128]{1,0:T(4,128)S(1)} %copy-done.84, bf16[128,3,64]{0,2,1:T(8,128)(2,1)S(1)} %bitcast.256, f32[6312,3,64]{0,2,1:T(8,128)} %bitcast.227, f32[3,64]{1,0:T(4,128)S(1)} %copy-done.93), kind=kOutput, calls=%fused_computation.16 | convolution fusion | flops 319942272 | bytes 24291072 | tf_op jit(solution)/shard_map/while/body/eval_jaxpr/qhe,khe->hqk/dot_general | solution.py:88
  448.1 12.9 %fusion.11 = f32[2,192,768]{2,1,0:T(8,128)} fusion(bf16[1,6312,1,192]{1,3,2,0:T(8,128)(2,1)} %bitcast.228, bf16[1,6312,1,192]{1,3,2,0:T(8,128)(2,1)} %bitcast.222, bf16[1,6312,768]{2,1,0:T(8,128)(2,1)} %dynamic_update_slice.42, f32[768]{0:T(1024)S(1)} %copy-done.89, f32[768]{0:T(1024)S(1)} %copy-done.45, f32[6312]{0:T(1024)S(1)} %copy-done.43, ...), kind=kOutput, calls=%fused_computation.21 | convolution fusion | flops 3754478592 | bytes 15779136 | tf_op jit(solution)/shard_map/cld,clkw->kwd/dot_general | solution.py:294
  490.7 16.4 %copy.51 = bf16[1,6312,2,192]{3,2,0,1:T(2,128)(2,1)} copy(bf16[1,6312,2,192]{1,3,2,0:T(8,128)(2,1)} %pad_maximum_fusion) | data formatting | bytes 9695232 | tf_op jit(solution)/shard_map/stack | solution.py:293
  532.7 64.0 %reduce-scatter.28.cloned.1.call-done = f32[96,192]{1,0:T(8,128)} async-done(((f32[768,192]{1,0:T(8,128)}), f32[96,192]{1,0:T(8,128)}) %reduce-scatter.28.cloned.1.call-update) | async-done | bytes 73744
  598.3 63.8 %reduce-scatter.32.cloned.1.call-done = f32[96,192]{1,0:T(8,128)} async-done(((f32[768,192]{1,0:T(8,128)}), f32[96,192]{1,0:T(8,128)}) %reduce-scatter.32.cloned.1.call-update) | async-done | bytes 73744
  663.8 65.6 %reduce-scatter.30.cloned.1.call-done = f32[96,384]{1,0:T(8,128)} async-done(((f32[768,384]{1,0:T(8,128)}), f32[96,384]{1,0:T(8,128)}) %reduce-scatter.30.cloned.1.call-update) | async-done | bytes 147472
  731.3 68.5 %reduce-scatter.34.cloned.1.call-done = f32[96,576]{1,0:T(8,128)} async-done(((f32[768,576]{1,0:T(8,128)}), f32[96,576]{1,0:T(8,128)}) %reduce-scatter.34.cloned.1.call-update) | async-done | bytes 221200
  801.8 17.3 %copy.52 = bf16[1,4,1578,2,192]{2,4,1,3,0:T(8,128)(2,1)} copy(bf16[1,4,1578,2,192]{4,3,2,1,0:T(2,128)(2,1)} %bitcast.46) | data formatting | bytes 9695232 | tf_op jit(solution)/shard_map/all_to_all | solution.py:298
  842.8 37.9 %all-reduce.1 = (f32[2,2,192]{2,1,0:T(2,128)}, f32[2,768]{1,0:T(2,128)}, f32[2,2,192]{2,1,0:T(2,128)}, f32[5,192]{1,0:T(8,128)}, f32[5,192]{1,0:T(8,128)}) all-reduce(f32[2,2,192]{2,1,0:T(2,128)S(1)} %pad_maximum_fusion.2, f32[2,768]{1,0:T(2,128)S(1)} %pad_maximum_fusion.1, ...), channel_id=1, replica_groups=mesh['dp'=8,'head'=4] {'dp'}, use_global_device_ids=true, to_apply=%region_47.48 | all-reduce | flops 4992 | bytes 39936 | tf_op jit(solution)/shard_map/psum | solution.py:329
  885.9 12.3 %reduce-scatter.24.cloned.1.call-done = f32[96,768]{1,0:T(8,128)} async-done(((f32[768,768]{1,0:T(8,128)}), f32[96,768]{1,0:T(8,128)}) %reduce-scatter.24.cloned.1.call-update) | async-done | bytes 294928 | tf_op jit(solution)/shard_map/reduce_scatter | solution.py:340
  898.2 72.9 %reduce-scatter.26.cloned.1.call-done = f32[768,96]{0,1:T(8,128)} async-done(((f32[768,768]{0,1:T(8,128)}), f32[768,96]{0,1:T(8,128)}) %reduce-scatter.26.cloned.1.call-update) | async-done | bytes 294928 | tf_op jit(solution)/shard_map/reduce_scatter | solution.py:341
  971.2 73.0 %reduce-scatter.20.cloned.1.call-done = f32[96,768]{1,0:T(8,128)} async-done(((f32[768,768]{1,0:T(8,128)}), f32[96,768]{1,0:T(8,128)}) %reduce-scatter.20.cloned.1.call-update) | async-done | bytes 294928 | tf_op jit(solution)/shard_map/reduce_scatter | solution.py:336
  1044.1 72.9 %reduce-scatter.22.cloned.1.call-done = f32[768,96]{0,1:T(8,128)} async-done(((f32[768,768]{0,1:T(8,128)}), f32[768,96]{0,1:T(8,128)}) %reduce-scatter.22.cloned.1.call-update) | async-done | bytes 294928 | tf_op jit(solution)/shard_map/reduce_scatter | solution.py:337
  (389 shorter events, 227.7 us)
Async XLA Ops:
  7.2 186.9 %copy-start = (bf16[768,768]{1,0:T(8,128)(2,1)S(1)}, bf16[768,768]{1,0:T(8,128)(2,1)}, u32[]{:S(2)}) copy-start(bf16[768,768]{1,0:T(8,128)(2,1)} %param.27) | copy-start | bytes 3538948
  7.2 182.4 %all-reduce.12.cloned.1.call-start = ((), (), s32[]{:S(2)}) async-start(), calls=%async_computation.10 | async-start | bytes 393216 | tf_op jit(solution)/shard_map/psum | solution.py:57
  7.3 53.6 %collective-permute-start = (bf16[1,1578,768]{2,1,0:T(8,128)(2,1)}, bf16[1,1578,768]{2,1,0:T(8,128)(2,1)}, u32[]{:S(2)}, u32[]{:S(2)}) collective-permute-start(bf16[1,1578,768]{2,1,0:T(8,128)(2,1)} %param.19), channel_id=1, source_target_pairs={{0,1},{1,2},{2,3},{3,0},{4,5},{5,6},{6,7},{7,4},{8,9},{9,10},{10,1... | collective-permute-start | bytes 7271432 | tf_op jit(solution)/shard_map/ppermute | solution.py:23
  7.8 88.3 %collective-permute-start.1 = (bf16[1,1578,768]{2,1,0:T(8,128)(2,1)}, bf16[1,1578,768]{2,1,0:T(8,128)(2,1)}, u32[]{:S(2)}, u32[]{:S(2)}) collective-permute-start(bf16[1,1578,768]{2,1,0:T(8,128)(2,1)} %param.19), channel_id=1, source_target_pairs={{0,3},{1,0},{2,1},{3,2},{4,7},{5,4},{6,5},{7,6},{8,11},{9,8},{10,9... | collective-permute-start | bytes 7271432 | tf_op jit(solution)/shard_map/ppermute | solution.py:28
  60.8 47.9 %collective-permute-start.2 = (bf16[1,1578,768]{2,1,0:T(8,128)(2,1)}, bf16[1,1578,768]{2,1,0:T(8,128)(2,1)}, u32[]{:S(2)}, u32[]{:S(2)}) collective-permute-start(bf16[1,1578,768]{2,1,0:T(8,128)(2,1)} %collective-permute-done), channel_id=1, source_target_pairs={{0,1},{1,2},{2,3},{3,0},{4,5},{5,6},{6,7},{7,4},{8,9},{9,10},{10,1... | collective-permute-start | bytes 7271432 | tf_op jit(solution)/shard_map/ppermute | solution.py:23
  83.2 108.7 %copy-start.47 = (f32[768]{0:T(1024)}, f32[768]{0:T(1024)S(1)}, u32[]{:S(2)}) copy-start(f32[768]{0:T(1024)S(1)} %get-tuple-element.151) | copy-start | bytes 9220
  155.8 71.5 %all-reduce.14.cloned.1.call-start = ((), (), s32[]{:S(2)}) async-start(), calls=%async_computation.11 | async-start | bytes 393216 | tf_op jit(solution)/shard_map/psum | solution.py:57
  195.1 74.1 %all-reduce.16.cloned.1.call-start = ((), (), s32[]{:S(2)}) async-start(), calls=%async_computation.12 | async-start | bytes 393216 | tf_op jit(solution)/shard_map/psum | solution.py:57
  237.0 72.7 %all-reduce.18.cloned.1.call-start = ((), (), s32[]{:S(2)}) async-start(), calls=%async_computation.13 | async-start | bytes 393216 | tf_op jit(solution)/shard_map/psum | solution.py:61
  277.5 80.8 %all-reduce.20.cloned.1.call-start = ((), (), s32[]{:S(2)}) async-start(), calls=%async_computation.14 | async-start | bytes 393216 | tf_op jit(solution)/shard_map/psum | solution.py:61
  326.1 72.9 %all-reduce.22.cloned.1.call-start = ((), (), s32[]{:S(2)}) async-start(), calls=%async_computation.15 | async-start | bytes 393216 | tf_op jit(solution)/shard_map/psum | solution.py:61
  366.8 148.9 %all-reduce.24.cloned.1.call-start = ((), (), s32[]{:S(2)}) async-start(), calls=%async_computation.26 | async-start | bytes 786432 | tf_op jit(solution)/shard_map/psum | solution.py:57
  431.4 99.7 %reduce-scatter.36.cloned.1.call-start = ((), (), s32[]{:S(2)}) async-start(), calls=%async_computation.25 | async-start | bytes 884736
  432.7 164.0 %reduce-scatter.28.cloned.1.call-start = ((), (), s32[]{:S(2)}) async-start(), calls=%async_computation.21 | async-start | bytes 884736
  440.8 221.3 %reduce-scatter.32.cloned.1.call-start = ((), (), s32[]{:S(2)}) async-start(), calls=%async_computation.23 | async-start | bytes 884736
  447.9 281.5 %reduce-scatter.30.cloned.1.call-start = ((), (), s32[]{:S(2)}) async-start(), calls=%async_computation.22 | async-start | bytes 1327104
  467.8 332.0 %reduce-scatter.34.cloned.1.call-start = ((), (), s32[]{:S(2)}) async-start(), calls=%async_computation.24 | async-start | bytes 2211840
  478.6 345.8 %all-gather.2.cloned.1.call-start = ((), (), s32[]{:S(2)}) async-start(), calls=%async_computation.16 | async-start | bytes 2949120 | tf_op jit(solution)/shard_map/all_gather | solution.py:168
  479.4 418.9 %reduce-scatter.24.cloned.1.call-start = ((), (), s32[]{:S(2)}) async-start(), calls=%async_computation.19 | async-start | bytes 2654208 | tf_op jit(solution)/shard_map/reduce_scatter | solution.py:340
  481.4 489.7 %reduce-scatter.26.cloned.1.call-start = ((), (), s32[]{:S(2)}) async-start(), calls=%async_computation.20 | async-start | bytes 2654208 | tf_op jit(solution)/shard_map/reduce_scatter | solution.py:341
  483.5 560.6 %reduce-scatter.20.cloned.1.call-start = ((), (), s32[]{:S(2)}) async-start(), calls=%async_computation.17 | async-start | bytes 2654208 | tf_op jit(solution)/shard_map/reduce_scatter | solution.py:336
  507.2 294.6 %all-to-all-start = ((bf16[1,6312,2,192]{3,2,0,1:T(2,128)(2,1)}), bf16[1,6312,2,192]{3,2,0,1:T(2,128)(2,1)}, u32[]{:S(2)}, u32[]{:S(2)}) async-start(bf16[1,6312,2,192]{3,2,0,1:T(2,128)(2,1)} %copy.51), calls=%async_computation | async-start | bytes 12926976 | tf_op jit(solution)/shard_map/all_to_all | solution.py:298
  512.6 604.4 %reduce-scatter.22.cloned.1.call-start = ((), (), s32[]{:S(2)}) async-start(), calls=%async_computation.18 | async-start | bytes 2654208 | tf_op jit(solution)/shard_map/reduce_scatter | solution.py:337
  880.7 236.4 %copy-start.1 = (bf16[768,768]{1,0:T(8,128)(2,1)S(1)}, bf16[768,768]{1,0:T(8,128)(2,1)}, u32[]{:S(2)}) copy-start(bf16[768,768]{1,0:T(8,128)(2,1)} %param.27) | copy-start | bytes 3538948
  (99 other events, 1879.7 us)
Sparse Core Ops, SparseCore 0:
  155.9 33.7 all-reduce.11
  195.2 32.0 all-reduce.13
  237.1 32.0 all-reduce.15
  277.6 32.0 all-reduce.17
  326.2 32.0 all-reduce.19
  367.0 32.0 all-reduce.21
  431.5 32.8 all-reduce.23
  467.7 63.2 reduce-scatter.35
  534.4 62.2 reduce-scatter.27
  599.8 62.2 reduce-scatter.31
  665.5 63.8 reduce-scatter.29
  733.3 66.4 reduce-scatter.33
  801.4 23.0 all-gather.1
  828.3 69.8 reduce-scatter.23
  902.2 68.9 reduce-scatter.25
  975.1 68.9 reduce-scatter.19
  1048.0 68.9 reduce-scatter.21
